TPU v7x, 512 devices: a whole 4x8x8 slice. The times are simulated.
512 devices in a mesh: op: 32 (over x, y_hi, core), sec: 16 (over z, y_lo).
Axes of the slice: x: 4, y: 8 (y_hi: 4, y_lo: 2; y = y_hi * 2 + y_lo), z: 8, core: 2. Of those that a mesh axis runs over, the one named last changes fastest.
Arguments:
- psi: bfloat16 [32, 512, 512], P('sec', 'op'), may hold values from -6 to 6
- left_ops: bfloat16 [64, 32, 512, 512], P('op', 'sec'), may hold values from -0.25 to 0.25
- right_ops: bfloat16 [64, 32, 512, 512], P('op', 'sec'), may hold values from -0.03125 to 0.03125
- conn: int32 [64, 32], P('op', 'sec'), may hold values from 0 to 31, as said below
- dims: int32 [32], P('sec'), may hold values from 128 to 512
Outputs:
- sigma: bfloat16 [32, 512, 512], P('sec', 'op')
Inputs may be any that keep to these rules, and one draw needn't show every extreme that they name: conn[k, s] lies in the same group of 2 consecutive sectors as s or in the next group, cyclically over the 32 sectors; both occur.
All inputs are finite; a program needn't handle non-finite values.
Results may differ from a plain program's by a relative error of at most 0.0049.
Values may be sent and summed in bfloat16 or wider, within the bound.
No kernel may reach another device: no remote copies, remote signals or barrier semaphores. Data moves between devices by JAX's collectives and lax.ppermute only.
A program may use at most 64 MiB of HBM per device.

v0:
```python
import jax
import jax.numpy as jnp
from jax import lax
from jax.sharding import Mesh
from jax.sharding import PartitionSpec as P

OP = ("op_0", "op_1", "op_2")


def in_blocks(x, dim, count):
    before, after = (x.shape[:dim], x.shape[dim + 1 :])
    return jnp.moveaxis(x.reshape(*before, count, -1, *after), dim, 0)


def sent_and_summed(x, axis, dim):
    tiles = in_blocks(x, dim, lax.axis_size(axis))
    arrived = lax.all_to_all(tiles, axis, split_axis=0, concat_axis=0, tiled=True)
    return arrived.sum(axis=0)


def sum_in_two_steps(x, axes, dim):
    far, near = axes
    tiles = in_blocks(x, dim, lax.axis_size(far))
    nearer = sent_and_summed(tiles, near, dim + 1)
    arrived = lax.all_to_all(nearer, far, split_axis=0, concat_axis=0, tiled=True)
    return arrived.sum(axis=0)


def side_by_side(arrays, axis, dim, along):
    widths = [a.shape[along] for a in arrays]
    both = jnp.concatenate(arrays, axis=along)
    whole = sum_in_two_steps(both, axis, dim)
    return tuple(jnp.split(whole, [sum(widths[:k]) for k in range(1, len(widths))], axis=along))


def from_behind(block, axis, distance):
    devices = range(lax.axis_size(axis))
    route = [((i - distance) % len(devices), i) for i in devices]
    return lax.ppermute(block, axis, route)


def row_mask(dims, row_start, rows, width):
    row_ids = row_start + jnp.arange(rows, dtype=jnp.int32)
    col_ids = jnp.arange(width, dtype=jnp.int32)
    return (row_ids[None, :, None] < dims[:, None, None]) & (
        col_ids[None, None, :] < dims[:, None, None]
    )


def on_device(psi, left_ops, right_ops, conn, dims):
    sdev, rows, width = psi.shape
    row_start = lax.axis_index(OP) * rows
    masked = jnp.where(row_mask(dims, row_start, rows, width), psi, jnp.zeros_like(psi))
    gathered = lax.all_gather(masked, OP, axis=1, tiled=True)
    half = jnp.einsum(
        "ksij,sjm->ksim", left_ops, gathered, preferred_element_type=jnp.float32
    ).astype(jnp.bfloat16)
    term = jnp.einsum("ksim,ksnm->ksin", half, right_ops, preferred_element_type=jnp.float32)
    group = lax.axis_index("sec")
    slot = conn % sdev
    elsewhere = conn // sdev != group
    slots = jnp.arange(sdev, dtype=jnp.int32)
    hits = slot[:, :, None] == slots[None, None, :]
    own_hot = (hits & ~elsewhere[:, :, None]).astype(jnp.float32)
    next_hot = (hits & elsewhere[:, :, None]).astype(jnp.float32)
    own = jnp.einsum("kst,ksin->tin", own_hot, term, precision=lax.Precision.HIGHEST)
    onward = jnp.einsum("kst,ksin->tin", next_hot, term, precision=lax.Precision.HIGHEST)
    own_rows, onward_rows = side_by_side((own, onward), (("op_0", "op_1"), "op_2"), 1, 0)
    summed = own_rows + from_behind(onward_rows, "sec", 1)
    summed = jnp.where(row_mask(dims, row_start, rows, width), summed, jnp.zeros_like(summed))
    return summed.astype(jnp.bfloat16)


def solution(mesh):
    finer = Mesh(mesh.devices.reshape(4, 4, 2, mesh.shape["sec"]), ("op_0", "op_1", "op_2", "sec"))
    in_specs = (
        P("sec", OP, None),
        P(OP, "sec", None, None),
        P(OP, "sec", None, None),
        P(OP, "sec"),
        P("sec"),
    )
    out_specs = P("sec", OP, None)
    return jax.shard_map(
        on_device, mesh=finer, in_specs=in_specs, out_specs=out_specs, check_vma=False
    )
```

profile of v0, /device:TPU:2, one launch (start us, length us, event | category | flops | bytes accessed | tf_op | source)
XLA Modules:
  0.0 198.4 jit_solution(11831326014869320493)
XLA Ops:
  6.5 0.0 copy-start
  6.5 0.0 all-gather.2.cloned.1.call-start
  6.5 0.9 iota_compare_fusion
  7.4 0.7 broadcast_compare_fusion.2
  8.1 1.4 and_select_fusion.1
  9.6 0.0 all-gather.2.cloned.1.call-update
  9.6 0.7 and_select_fusion.3
  10.3 0.7 fusion.27
  11.0 60.2 %all-gather.2.cloned.1.call-done = bf16[2,512,512]{2,1,0:T(8,128)(2,1)} async-done(((bf16[2,16,512]{2,1,0:T(8,128)(2,1)}), bf16[2,512,512]{2,1,0:T(8,128)(2,1)}) %all-gather.2.cloned.1.call-update) | async-done | bytes 1048592 | tf_op jit(solution)/shard_map/all_gather | solution.py:54
  71.2 0.0 copy-done
  71.2 6.4 %fusion.4 = f32[2,2,512,512]{3,2,1,0:T(8,128)} fusion(bf16[2,2,512,512]{3,2,1,0:T(8,128)(2,1)S(1)} %copy-done, bf16[2,2,512,512]{3,2,1,0:T(8,128)(2,1)} %param.6, bf16[2,512,512]{2,1,0:T(8,128)(2,1)} %all-gather.2.cloned.1.call-done), kind=kOutput, calls=%fused_computation.5 | convolution fusion | flops 2148532224 | bytes 9437184 | tf_op jit(solution)/shard_map/ksim,ksnm->ksin/dot_general | solution.py:58
  77.6 0.0 copy-start.1
  77.6 14.6 %fusion.12 = f32[2,512,512]{2,0,1:T(2,128)S(1)} fusion(f32[2,2,512,512]{3,2,1,0:T(8,128)} %fusion.4, pred[2,2]{1,0:T(4,128)(4,1)S(1)} %get-tuple-element.6, s32[2,2]{1,0:T(2,128)S(1)} %and_select_fusion.3), kind=kOutput, calls=%fused_computation.10 | convolution fusion | flops 25165840 | bytes 6291476 | tf_op jit(solution)/shard_map/kst,ksin->tin/dot_general | solution.py:67
  92.2 0.0 copy-done.1
  92.2 9.7 %fusion.9 = f32[2,512,512]{2,0,1:T(2,128)S(1)} fusion(f32[2,2,512,512]{3,2,1,0:T(8,128)S(1)} %copy-done.1, pred[2,2]{1,0:T(4,128)(4,1)S(1)} %get-tuple-element.5, s32[2,2]{1,0:T(2,128)S(1)} %and_select_fusion.3), kind=kOutput, calls=%fused_computation.9 | convolution fusion | flops 25165840 | bytes 6291476 | tf_op jit(solution)/shard_map/kst,ksin->tin/dot_general | solution.py:66
  101.9 1.9 pad_maximum_fusion
  103.8 1.3 copy.20
  105.1 3.6 %copy.21 = f32[2,16,4,16,512]{4,2,3,1,0:T(4,128)S(1)} copy(f32[2,16,4,16,512]{4,3,0,2,1:T(8,128)S(1)} %bitcast.28) | data formatting | bytes 8388608 | tf_op jit(solution)/shard_map/transpose | solution.py:12
  108.7 8.2 %all_to_all.10 = f32[2,16,4,16,512]{4,2,3,1,0:T(4,128)} all-to-all(f32[2,16,4,16,512]{4,2,3,1,0:T(4,128)S(1)} %copy.21), channel_id=1, replica_groups=mesh['op_0'=4,'op_1'=4,'op_2'=2,'sec'=16] {'op_2'}, dimensions={0} | all-to-all | bytes 8388608 | tf_op jit(solution)/shard_map/all_to_all | solution.py:17
  116.8 5.3 %reduce_sum.18 = f32[16,4,16,512]{3,1,2,0:T(4,128)} reduce(f32[2,16,4,16,512]{4,2,3,1,0:T(4,128)} %all_to_all.10, f32[]{:T(128)} %constant.53.clone.1), dimensions={0}, to_apply=%region_0.1 | reduce | flops 524288 | bytes 6291460 | tf_op jit(solution)/shard_map/reduce_sum | solution.py:18
  122.1 58.1 %all_to_all.11 = f32[16,4,16,512]{3,1,2,0:T(4,128)} all-to-all(f32[16,4,16,512]{3,1,2,0:T(4,128)} %reduce_sum.18), channel_id=1, replica_groups=mesh['op_0'=4,'op_1'=4,'op_2'=2,'sec'=16] {'op_0','op_1'}, dimensions={0} | all-to-all | bytes 4194304 | tf_op jit(solution)/shard_map/all_to_all | solution.py:25
  180.3 1.9 reduce_sum.19
  182.2 0.1 fusion.29
  182.3 3.0 %collective-permute-start = (f32[2,16,512]{2,1,0:T(8,128)S(1)}, f32[2,16,512]{2,1,0:T(8,128)S(1)}, u32[]{:S(2)}, u32[]{:S(2)}) collective-permute-start(f32[2,16,512]{2,1,0:T(8,128)S(1)} %copy.30), channel_id=1, source_target_pairs={{15,0},{0,1},{1,2},{2,3},{3,4},{4,5},{5,6},{6,7},{7,8},{8,9},{9,10... | collective-permute-start | bytes 196616 | tf_op jit(solution)/shard_map/ppermute | solution.py:39
  185.3 5.6 %collective-permute-done = f32[2,16,512]{2,1,0:T(8,128)S(1)} collective-permute-done((f32[2,16,512]{2,1,0:T(8,128)S(1)}, f32[2,16,512]{2,1,0:T(8,128)S(1)}, u32[]{:S(2)}, u32[]{:S(2)}) %collective-permute-start) | collective-permute-done | bytes 65568 | tf_op jit(solution)/shard_map/ppermute | solution.py:39
  190.9 0.7 fusion.17
  (2 shorter events, 0.0 us)
Async XLA Ops:
  6.5 64.7 %copy-start = (bf16[2,2,512,512]{3,2,1,0:T(8,128)(2,1)S(1)}, bf16[2,2,512,512]{3,2,1,0:T(8,128)(2,1)}, u32[]{:S(2)}) copy-start(bf16[2,2,512,512]{3,2,1,0:T(8,128)(2,1)} %param.7) | copy-start | bytes 6291460
  6.5 64.7 %all-gather.2.cloned.1.call-start = ((), (), s32[]{:S(2)}) async-start(), calls=%async_computation.2 | async-start | bytes 1081344 | tf_op jit(solution)/shard_map/all_gather | solution.py:54
  77.6 14.6 %copy-start.1 = (f32[2,2,512,512]{3,2,1,0:T(8,128)S(1)}, f32[2,2,512,512]{3,2,1,0:T(8,128)}, u32[]{:S(2)}) copy-start(f32[2,2,512,512]{3,2,1,0:T(8,128)} %fusion.4) | copy-start | bytes 12582916
  182.3 8.6 %collective-permute-start = (f32[2,16,512]{2,1,0:T(8,128)S(1)}, f32[2,16,512]{2,1,0:T(8,128)S(1)}, u32[]{:S(2)}, u32[]{:S(2)}) collective-permute-start(f32[2,16,512]{2,1,0:T(8,128)S(1)} %copy.30), channel_id=1, source_target_pairs={{15,0},{0,1},{1,2},{2,3},{3,4},{4,5},{5,6},{6,7},{7,8},{8,9},{9,10... | collective-permute-start | bytes 196616 | tf_op jit(solution)/shard_map/ppermute | solution.py:39
Sparse Core Ops, SparseCore 0:
  10.6 60.6 all-gather.1
where the time goes:
time: 199 us; the launch traced here: 198 us
  blocking collectives  66.3 us (33%)
  waiting for transfers between devices  65.9 us (33%)
  matrix products  30.6 us (15%)
  other arithmetic  14.2 us (7%)
  between operations  13.5 us (7%)
  local copies, waits for them, and re-layouts  4.98 us (3%)
  starting transfers between devices  3 us (2%)
    all_gather x1, waiting for transfers between devices, on_device(): gathered = lax.all_gather(masked, OP, axis=1, tiled=True)  60.2 us
    all_to_all x1, blocking collectives, sum_in_two_steps(): lax.all_to_all(nearer, far, split_axis=0, concat_axis=0, tiled=True)  58.1 us
    dot_general x1, matrix products, on_device(): jnp.einsum('kst,ksin->tin', next_hot, term, precision=lax.Precision.HIGHEST)  14.6 us
    dot_general x1, matrix products, on_device(): jnp.einsum('kst,ksin->tin', own_hot, term, precision=lax.Precision.HIGHEST)  9.66 us
    all_to_all x1, blocking collectives, sent_and_summed(): lax.all_to_all(tiles, axis, split_axis=0, concat_axis=0, tiled=True)  8.16 us
    dot_general x1, matrix products, on_device(): jnp.einsum('ksim,ksnm->ksin', half, right_ops, preferred_element_type=jnp...  6.38 us
    ppermute x1, waiting for transfers between devices, from_behind(): return lax.ppermute(block, axis, route)  5.62 us
    reduce_sum x1, other arithmetic, sent_and_summed(): return arrived.sum(axis=0)  5.27 us
  transfers between devices with their start and end apart: 2, of which 2 were waited for; matrix products, arithmetic and copies ran while one was open for 1% of the time, Pallas kernels for 0%

commit v1 on v0

--- a/solution.py
+++ b/solution.py
@@ -51,7 +51,10 @@
     sdev, rows, width = psi.shape
     row_start = lax.axis_index(OP) * rows
     masked = jnp.where(row_mask(dims, row_start, rows, width), psi, jnp.zeros_like(psi))
-    gathered = lax.all_gather(masked, OP, axis=1, tiled=True)
+    devices_2 = lax.axis_size(OP)
+    blocks = jnp.stack([masked for _ in range(devices_2)])
+    blocks = lax.all_to_all(blocks, OP, split_axis=0, concat_axis=0)
+    gathered = jnp.concatenate(blocks, axis=1)
     half = jnp.einsum(
         "ksij,sjm->ksim", left_ops, gathered, preferred_element_type=jnp.float32
     ).astype(jnp.bfloat16)

time: 199 us -> 167 us (0.84)
  waiting for transfers between devices: 65.9 us -> 38 us
  between operations: 13.5 us -> 0.12 us
  starting transfers between devices: 3 us -> 13.5 us
  local copies, waits for them, and re-layouts: 4.98 us -> 7.73 us
  other arithmetic: 14.2 us -> 11.7 us
    all_gather x1 -> x0, waiting for transfers between devices: 60.2 us -> none  [on_device(): gathered = lax.all_gather(masked, OP, axis=1, tiled=True)]
    all_to_all x0 -> x1, waiting for transfers between devices: none -> 27.3 us  [on_device(): blocks = lax.all_to_all(blocks, OP, split_axis=0, concat_axis=0)]
    all_to_all x0 -> x1, starting transfers between devices: none -> 10.3 us  [on_device(): blocks = lax.all_to_all(blocks, OP, split_axis=0, concat_axis=0)]
    ppermute x1, waiting for transfers between devices: 5.62 us -> 10.7 us  [from_behind(): return lax.ppermute(block, axis, route)]
  transfers between devices with their start and end apart: 2 -> 2, of which waited for: 2 -> 2; matrix products, arithmetic and copies ran while one was open for 1% -> 0% of each run, Pallas kernels for 0% -> 0%
where the time goes in v1:
time: 167 us
  blocking collectives  65.2 us (39%)
  waiting for transfers between devices  38 us (23%)
  matrix products  30.6 us (18%)
  starting transfers between devices  13.5 us (8%)
  other arithmetic  11.7 us (7%)
  local copies, waits for them, and re-layouts  7.73 us (5%)
    all_to_all x1, blocking collectives, sum_in_two_steps(): lax.all_to_all(nearer, far, split_axis=0, concat_axis=0, tiled=True)  56.4 us
    all_to_all x1, waiting for transfers between devices, on_device(): blocks = lax.all_to_all(blocks, OP, split_axis=0, concat_axis=0)  27.3 us
    dot_general x1, matrix products, on_device(): jnp.einsum('kst,ksin->tin', next_hot, term, precision=lax.Precision.HIGHEST)  14.6 us
    ppermute x1, waiting for transfers between devices, from_behind(): return lax.ppermute(block, axis, route)  10.7 us
    all_to_all x1, starting transfers between devices, on_device(): blocks = lax.all_to_all(blocks, OP, split_axis=0, concat_axis=0)  10.3 us
    dot_general x1, matrix products, on_device(): jnp.einsum('kst,ksin->tin', own_hot, term, precision=lax.Precision.HIGHEST)  9.64 us
    all_to_all x1, blocking collectives, sent_and_summed(): lax.all_to_all(tiles, axis, split_axis=0, concat_axis=0, tiled=True)  8.83 us
    dot_general x1, matrix products, on_device(): jnp.einsum('ksim,ksnm->ksin', half, right_ops, preferred_element_type=jnp...  6.38 us
  transfers between devices with their start and end apart: 2, of which 2 were waited for; matrix products, arithmetic and copies ran while one was open for 0% of the time, Pallas kernels for 0%

profile of v1, /device:TPU:2, one launch (start us, length us, event | category | flops | bytes accessed | tf_op | source)
XLA Modules:
  0.0 166.9 jit_solution(16191313170177686752)
XLA Ops:
  0.0 0.0 copy-start
  0.0 0.0 copy-start.1
  0.0 0.9 iota_compare_fusion
  0.9 0.7 broadcast_compare_fusion
  1.6 0.9 and_select_fusion.1
  2.5 1.1 stack.2
  3.6 10.3 %all-to-all-start = ((bf16[32,2,16,512]{3,2,1,0:T(8,128)(2,1)}), bf16[32,2,16,512]{3,2,1,0:T(8,128)(2,1)S(1)}, u32[]{:S(2)}, u32[]{:S(2)}) async-start(bf16[32,2,16,512]{3,2,1,0:T(8,128)(2,1)} %stack.2), calls=%async_computation | async-start | bytes 2097152 | tf_op jit(solution)/shard_map/all_to_all | solution.py:56
  13.9 0.0 copy-done.1
  13.9 27.3 %all-to-all-done = bf16[32,2,16,512]{3,2,1,0:T(8,128)(2,1)S(1)} async-done(((bf16[32,2,16,512]{3,2,1,0:T(8,128)(2,1)}), bf16[32,2,16,512]{3,2,1,0:T(8,128)(2,1)S(1)}, u32[]{:S(2)}, u32[]{:S(2)}) %all-to-all-start) | async-done | bytes 1048608 | tf_op jit(solution)/shard_map/all_to_all | solution.py:56
  41.2 1.0 copy.26
  42.3 0.0 copy-done
  42.3 6.4 %fusion.4 = f32[2,2,512,512]{3,2,1,0:T(8,128)} fusion(bf16[2,2,512,512]{3,2,1,0:T(8,128)(2,1)S(1)} %copy-done, bf16[2,512,512,1]{2,1,0,3:T(8,128)(2,1)} %bitcast.31, bf16[2,2,512,512]{3,2,1,0:T(8,128)(2,1)} %param.6), kind=kOutput, calls=%fused_computation.5 | convolution fusion | flops 2148532224 | bytes 9437184 | tf_op jit(solution)/shard_map/ksim,ksnm->ksin/dot_general | solution.py:61
  48.7 0.0 copy-start.2
  48.7 14.6 %fusion.12 = f32[2,512,512]{2,0,1:T(2,128)S(1)} fusion(f32[2,2,512,512]{3,2,1,0:T(8,128)} %fusion.4, pred[2,2]{1,0:T(4,128)(4,1)S(1)} %get-tuple-element.6, s32[2,2]{1,0:T(2,128)S(1)} %and_select_fusion.3), kind=kOutput, calls=%fused_computation.10 | convolution fusion | flops 25165840 | bytes 6291476 | tf_op jit(solution)/shard_map/kst,ksin->tin/dot_general | solution.py:70
  63.2 0.0 copy-done.2
  63.2 9.6 %fusion.9 = f32[2,512,512]{2,0,1:T(2,128)S(1)} fusion(f32[2,2,512,512]{3,2,1,0:T(8,128)S(1)} %copy-done.2, pred[2,2]{1,0:T(4,128)(4,1)S(1)} %get-tuple-element.5, s32[2,2]{1,0:T(2,128)S(1)} %and_select_fusion.3), kind=kOutput, calls=%fused_computation.9 | convolution fusion | flops 25165840 | bytes 6291476 | tf_op jit(solution)/shard_map/kst,ksin->tin/dot_general | solution.py:69
  72.9 1.9 %pad_maximum_fusion = f32[4,512,512]{2,0,1:T(4,128)S(1)} fusion(f32[2,512,512]{2,0,1:T(2,128)S(1)} %fusion.12, f32[2,512,512]{2,0,1:T(2,128)S(1)} %fusion.9), kind=kLoop, calls=%fused_computation | loop fusion | flops 1048576 | bytes 8388608 | tf_op jit(solution)/shard_map/concatenate | solution.py:31
  74.8 1.3 copy.31
  76.1 3.6 %copy.32 = f32[2,16,4,16,512]{4,2,3,1,0:T(4,128)S(1)} copy(f32[2,16,4,16,512]{4,3,0,2,1:T(8,128)S(1)} %bitcast.30) | data formatting | bytes 8388608 | tf_op jit(solution)/shard_map/transpose | solution.py:12
  79.7 8.8 %all_to_all.15 = f32[2,16,4,16,512]{4,2,3,1,0:T(4,128)} all-to-all(f32[2,16,4,16,512]{4,2,3,1,0:T(4,128)S(1)} %copy.32), channel_id=1, replica_groups=mesh['op_0'=4,'op_1'=4,'op_2'=2,'sec'=16] {'op_2'}, dimensions={0} | all-to-all | bytes 8388608 | tf_op jit(solution)/shard_map/all_to_all | solution.py:17
  88.5 5.3 %reduce_sum.18 = f32[16,4,16,512]{3,1,2,0:T(4,128)} reduce(f32[2,16,4,16,512]{4,2,3,1,0:T(4,128)} %all_to_all.15, f32[]{:T(128)} %constant.53.clone.1), dimensions={0}, to_apply=%region_0.1 | reduce | flops 524288 | bytes 6291460 | tf_op jit(solution)/shard_map/reduce_sum | solution.py:18
  93.8 56.4 %all_to_all.16 = f32[16,4,16,512]{3,1,2,0:T(4,128)} all-to-all(f32[16,4,16,512]{3,1,2,0:T(4,128)} %reduce_sum.18), channel_id=1, replica_groups=mesh['op_0'=4,'op_1'=4,'op_2'=2,'sec'=16] {'op_0','op_1'}, dimensions={0} | all-to-all | bytes 4194304 | tf_op jit(solution)/shard_map/all_to_all | solution.py:25
  150.2 1.9 %reduce_sum.19 = f32[4,16,512]{2,0,1:T(4,128)S(1)} reduce(f32[16,4,16,512]{3,1,2,0:T(4,128)} %all_to_all.16, f32[]{:T(128)} %constant.53.clone.1), dimensions={0}, to_apply=%region_1.2 | reduce | flops 491520 | bytes 2228228 | tf_op jit(solution)/shard_map/reduce_sum | solution.py:26
  152.1 3.3 %collective-permute-start = (f32[2,16,512]{2,0,1:T(2,128)S(1)}, f32[2,16,512]{2,0,1:T(2,128)S(1)}, u32[]{:S(2)}, u32[]{:S(2)}) collective-permute-start(f32[2,16,512]{2,0,1:T(2,128)S(1)} %split.9), channel_id=1, source_target_pairs={{15,0},{0,1},{1,2},{2,3},{3,4},{4,5},{5,6},{6,7},{7,8},{8,9},{9,10... | collective-permute-start | bytes 196616 | tf_op jit(solution)/shard_map/ppermute | solution.py:39
  155.4 10.7 %collective-permute-done = f32[2,16,512]{2,0,1:T(2,128)S(1)} collective-permute-done((f32[2,16,512]{2,0,1:T(2,128)S(1)}, f32[2,16,512]{2,0,1:T(2,128)S(1)}, u32[]{:S(2)}, u32[]{:S(2)}) %collective-permute-start) | collective-permute-done | bytes 65568 | tf_op jit(solution)/shard_map/ppermute | solution.py:39
  166.1 0.1 fusion.15
  166.2 0.6 copy.34
  (5 shorter events, 0.1 us)
Async XLA Ops:
  0.0 42.3 %copy-start = (bf16[2,2,512,512]{3,2,1,0:T(8,128)(2,1)S(1)}, bf16[2,2,512,512]{3,2,1,0:T(8,128)(2,1)}, u32[]{:S(2)}) copy-start(bf16[2,2,512,512]{3,2,1,0:T(8,128)(2,1)} %param.7) | copy-start | bytes 6291460
  0.0 13.9 %copy-start.1 = (s32[2,2]{1,0:T(2,128)S(1)}, s32[2,2]{1,0:T(2,128)}, u32[]{:S(2)}) copy-start(s32[2,2]{1,0:T(2,128)} %param.8) | copy-start | bytes 52
  3.6 37.6 %all-to-all-start = ((bf16[32,2,16,512]{3,2,1,0:T(8,128)(2,1)}), bf16[32,2,16,512]{3,2,1,0:T(8,128)(2,1)S(1)}, u32[]{:S(2)}, u32[]{:S(2)}) async-start(bf16[32,2,16,512]{3,2,1,0:T(8,128)(2,1)} %stack.2), calls=%async_computation | async-start | bytes 2097152 | tf_op jit(solution)/shard_map/all_to_all | solution.py:56
  48.7 14.6 %copy-start.2 = (f32[2,2,512,512]{3,2,1,0:T(8,128)S(1)}, f32[2,2,512,512]{3,2,1,0:T(8,128)}, u32[]{:S(2)}) copy-start(f32[2,2,512,512]{3,2,1,0:T(8,128)} %fusion.4) | copy-start | bytes 12582916
  152.1 14.0 %collective-permute-start = (f32[2,16,512]{2,0,1:T(2,128)S(1)}, f32[2,16,512]{2,0,1:T(2,128)S(1)}, u32[]{:S(2)}, u32[]{:S(2)}) collective-permute-start(f32[2,16,512]{2,0,1:T(2,128)S(1)} %split.9), channel_id=1, source_target_pairs={{15,0},{0,1},{1,2},{2,3},{3,4},{4,5},{5,6},{6,7},{7,8},{8,9},{9,10... | collective-permute-start | bytes 196616 | tf_op jit(solution)/shard_map/ppermute | solution.py:39
